TPU v7x, 32 devices: a whole 2x2x4 slice. The times are simulated.
32 devices in a mesh: gx: 8 (over z, x), gy: 4 (over y, core).
Axes of the slice: x: 2, y: 2, z: 4, core: 2. Of those that a mesh axis runs over, the one named last changes fastest.
Arguments:
- mode_fields: float32 [32, 512, 1024], P(None, 'gx', 'gy'), may hold values from -60 to 60, as said below
- conductance: float32 [512, 1024], P('gx', 'gy'), may hold values from 0.5 to 2
- potential: float32 [512, 1024], P('gx', 'gy'), may hold values from 0.25 to 4
Outputs:
- basis_field: float32 [128, 512, 1024], P(None, 'gx', 'gy')
- scaled_factor: float32 [128, 128], replicated
Inputs may be any that keep to these rules, and one draw needn't show every extreme that they name: `mode_fields`: Real-valued mode amplitudes.
All inputs are finite; a program needn't handle non-finite values.
Results may differ from a plain program's by a relative error of at most 0.0003.
Values sent between devices are 32-bit elements; how exact they have to be, the bound alone decides.
A program may use at most 64 MiB of HBM per device.

v0:
```python
import jax
import jax.numpy as jnp
from jax import lax
from jax.sharding import PartitionSpec as P


def padded_2(value, sides, width):
    for axis, dim in sides:
        peers, length = (lax.axis_size(axis), value.shape[dim])
        up = [(i, (i + 1) % peers) for i in range(peers - 1)]
        down = [(j, i) for i, j in up]
        last = lax.slice_in_dim(value, length - width, length, axis=dim)
        first = lax.slice_in_dim(value, 0, width, axis=dim)
        before = lax.ppermute(last, axis, up)
        after = lax.ppermute(first, axis, down)
        value = jnp.concatenate([before, value, after], axis=dim)
    return value


def build_columns(fields, conduct, potential):
    center = fields[:, 1:-1, 1:-1]
    k_mid = conduct[1:-1, 1:-1]
    x_plus = 0.5 * (k_mid + conduct[2:, 1:-1])
    x_minus = 0.5 * (k_mid + conduct[:-2, 1:-1])
    y_plus = 0.5 * (k_mid + conduct[1:-1, 2:])
    y_minus = 0.5 * (k_mid + conduct[1:-1, :-2])
    along_x = x_plus * (center - fields[:, 2:, 1:-1]) + x_minus * (center - fields[:, :-2, 1:-1])
    along_y = y_plus * (center - fields[:, 1:-1, 2:]) + y_minus * (center - fields[:, 1:-1, :-2])
    react = potential * center
    stacked = jnp.concatenate([center, along_x, along_y, react], 0)
    return stacked.reshape(stacked.shape[0], -1)


def inner_products(matrix, cell_count):
    return jnp.dot(matrix, matrix.T, precision=lax.Precision.HIGHEST) / cell_count


def on_device(mode_fields, conductance, potential):
    modes_count = mode_fields.shape[0]
    rows_here = mode_fields.shape[1]
    cols_here = mode_fields.shape[2]
    stacked = jnp.concatenate([mode_fields, conductance[None]], 0)
    padded = padded_2(stacked, (("gx", 1), ("gy", 2)), 1)
    matrix = build_columns(padded[:modes_count], padded[modes_count], potential)
    cell_count = float(rows_here * cols_here * lax.axis_size("gx") * lax.axis_size("gy"))
    gram_total = lax.psum(inner_products(matrix, cell_count), ("gx", "gy"))
    lower_tri = jnp.linalg.cholesky(gram_total)
    basis_flat = jax.scipy.linalg.solve_triangular(lower_tri, matrix, lower=True)
    basis_field = basis_flat.reshape(basis_flat.shape[0], rows_here, cols_here)
    return (basis_field, lower_tri.T)


def solution(mesh):
    placed = (P(None, "gx", "gy"), P("gx", "gy"), P("gx", "gy"))
    return jax.shard_map(
        on_device, mesh=mesh, in_specs=placed, out_specs=(P(None, "gx", "gy"), P()), check_vma=False
    )
```

profile of v0, /device:TPU:1, one launch (start us, length us, event | category | flops | bytes accessed | tf_op | source)
XLA Modules:
  0.0 232.6 jit_solution(10538956578714779694)
XLA Ops:
  7.2 0.9 broadcast_in_dim.3
  8.1 5.0 %fusion.22 = (f32[32,64,256]{2,0,1:T(8,128)}, f32[33,64,256]{2,0,1:T(8,128)S(1)}, f32[32,64,256]{2,0,1:T(8,128)}) fusion(f32[32,64,256]{2,1,0:T(8,128)} %param.3, f32[64,256]{1,0:T(8,128)} %param.5), kind=kLoop, calls=%fused_computation.51 | loop fusion | flops 524287 | bytes 8454144 | tf_op args[0]
  13.1 0.9 dynamic-update-slice.4
  14.0 3.9 %collective-permute-start = (f32[33,1,256]{2,0,1:T(8,128)S(1)}, f32[33,1,256]{2,0,1:T(8,128)S(1)}, u32[]{:S(2)}, u32[]{:S(2)}) collective-permute-start(f32[33,1,256]{2,0,1:T(8,128)S(1)} %get-tuple-element.12), channel_id=1, source_target_pairs={{0,4},{4,8},{8,12},{12,16},{16,20},{20,24},{24,28},{1,5},{5,9},{9,... | collective-permute-start | bytes 101384 | tf_op jit(solution)/shard_map/ppermute | solution.py:14
  17.9 1.3 collective-permute-start.1
  19.2 3.4 %collective-permute-done.1 = f32[33,1,256]{2,0,1:T(8,128)S(1)} collective-permute-done((f32[33,1,256]{2,0,1:T(8,128)S(1)}, f32[33,1,256]{2,0,1:T(8,128)S(1)}, u32[]{:S(2)}, u32[]{:S(2)}) %collective-permute-start.1) | collective-permute-done | bytes 33824 | tf_op jit(solution)/shard_map/ppermute | solution.py:15
  22.7 0.2 pad_maximum_fusion.1
  22.8 1.9 fusion.20
  24.8 1.8 copy.32
  26.6 4.0 %collective-permute-start.3 = (f32[33,66,1]{1,2,0:T(1,128)S(1)}, f32[33,66,1]{1,2,0:T(1,128)S(1)}, u32[]{:S(2)}, u32[]{:S(2)}) collective-permute-start(f32[33,66,1]{1,2,0:T(1,128)S(1)} %copy.32), channel_id=1, source_target_pairs={{1,0},{2,1},{3,2},{5,4},{6,5},{7,6},{9,8},{10,9},{11,10},{13,12},{... | collective-permute-start | bytes 26144 | tf_op jit(solution)/shard_map/ppermute | solution.py:15
  30.6 1.8 copy.31
  32.4 3.1 %collective-permute-start.2 = (f32[33,66,1]{1,2,0:T(1,128)S(1)}, f32[33,66,1]{1,2,0:T(1,128)S(1)}, u32[]{:S(2)}, u32[]{:S(2)}) collective-permute-start(f32[33,66,1]{1,2,0:T(1,128)S(1)} %copy.31), channel_id=1, source_target_pairs={{0,1},{1,2},{2,3},{4,5},{5,6},{6,7},{8,9},{9,10},{10,11},{12,13},{... | collective-permute-start | bytes 26144 | tf_op jit(solution)/shard_map/ppermute | solution.py:14
  35.4 1.7 copy.34
  37.1 1.7 copy.33
  38.8 1.5 pad_maximum_fusion.10
  40.3 0.1 fusion.16
  40.5 0.2 copy-done.1
  40.7 0.7 copy-done.2
  41.3 7.0 %fusion.9 = (f32[32,64,256]{2,0,1:T(8,128)}, f32[32,64,256]{2,0,1:T(8,128)}) fusion(f32[33,64,256]{2,0,1:T(8,128)S(1)} %dynamic-update-slice.4, f32[33,1,256]{2,0,1:T(8,128)S(1)} %collective-permute-done, f32[33,1,256]{2,0,1:T(8,128)S(1)} %collective-permute-done.1, f32[64,256]{1,0:T(8,128)S(1)} %get-tuple-element.19, f32[64,256]{1,0:T(8,128)S(1)} %get-tuple-element.17, ...), kind=kLoop, calls=%fused_computation.18 | loop fusion | flops 9437184 | bytes 8801296 | tf_op jit(solution)/shard_map/add | solution.py:27
  48.3 10.7 %fusion.12 = f32[128,128]{0,1:T(8,128)} fusion(f32[32,64,256]{2,0,1:T(8,128)} %get-tuple-element.16, f32[32,64,256]{2,0,1:T(8,128)} %get-tuple-element.9, f32[32,64,256]{2,0,1:T(8,128)} %get-tuple-element.8, f32[32,64,256]{2,0,1:T(8,128)S(1)} %copy-done.3), kind=kOutput, calls=%fused_computation.23 | convolution fusion | flops 3227533312 | bytes 8454144 | tf_op jit(solution)/shard_map/dot_general | solution.py:35
  59.0 5.7 %pad_maximum_fusion = f32[128,64,256]{2,0,1:T(8,128)} fusion(f32[32,64,256]{2,0,1:T(8,128)} %get-tuple-element.16, f32[32,64,256]{2,0,1:T(8,128)} %get-tuple-element.9, f32[32,64,256]{2,0,1:T(8,128)} %get-tuple-element.8, f32[32,64,256]{2,0,1:T(8,128)S(1)} %copy-done.4), kind=kLoop, calls=%fused_computation | loop fusion | flops 6291456 | bytes 16777216 | tf_op jit(solution)/shard_map/concatenate | solution.py:30
  64.7 9.0 %copy.45 = f32[128,64,256]{0,2,1:T(8,128)} copy(f32[128,64,256]{2,0,1:T(8,128)} %pad_maximum_fusion) | data formatting | bytes 16777216 | tf_op jit(solution)/shard_map/concatenate | solution.py:30
  73.7 107.6 %all-reduce.2.cloned.1.call-done = f32[128,128]{0,1:T(8,128)} async-done(((f32[128,128]{0,1:T(8,128)}), f32[128,128]{0,1:T(8,128)}) %all-reduce.2.cloned.1.call-update) | async-done | bytes 65552 | tf_op jit(solution)/shard_map/psum | solution.py:46
  181.3 0.9 copy.44
  182.3 0.9 fusion.18
  183.1 11.7 %cholesky.16 = f32[128,128]{1,0:T(8,128)S(1)} custom-call(f32[128,128]{1,0:T(8,128)S(1)} %fusion.18), custom_call_target="Cholesky" | custom-call | tf_op jit(solution)/shard_map/jit(cholesky)/cholesky | solution.py:47
  194.9 0.6 compare_reduce_fusion
  195.5 0.7 fusion.19
  196.2 0.7 copy.48
  196.9 9.8 %custom-call.7 = f32[1,128,128]{1,2,0:T(8,128)S(1)} custom-call(f32[1,128,128]{2,1,0:T(8,128)S(1)} %get-tuple-element.22), custom_call_target="InvertDiagBlocksLowerTriangular" | custom-call | tf_op jit(solution)/shard_map/jit(_solve_triangular)/triangular_solve | solution.py:48
  206.7 10.7 %fusion = f32[128,64,256]{2,0,1:T(8,128)S(1)} fusion(f32[128,64,256]{0,2,1:T(8,128)} %copy.45, f32[1,128,128]{1,2,0:T(8,128)S(1)} %custom-call.7), kind=kOutput, calls=%fused_computation.1 | convolution fusion | flops 3221225472 | bytes 16842752 | tf_op jit(solution)/shard_map/jit(_solve_triangular)/triangular_solve | solution.py:48
  217.5 8.3 %copy.47 = f32[128,64,256]{2,1,0:T(8,128)} copy(f32[128,64,256]{2,0,1:T(8,128)S(1)} %fusion) | data formatting | bytes 16777216
  (16 shorter events, 0.1 us)
Async XLA Ops:
  7.2 174.2 %all-reduce.2.cloned.1.call-start = ((), (), s32[]{:S(2)}) async-start(), calls=%async_computation | async-start | bytes 131072 | tf_op jit(solution)/shard_map/psum | solution.py:46
  14.0 5.2 %collective-permute-start = (f32[33,1,256]{2,0,1:T(8,128)S(1)}, f32[33,1,256]{2,0,1:T(8,128)S(1)}, u32[]{:S(2)}, u32[]{:S(2)}) collective-permute-start(f32[33,1,256]{2,0,1:T(8,128)S(1)} %get-tuple-element.12), channel_id=1, source_target_pairs={{0,4},{4,8},{8,12},{12,16},{16,20},{20,24},{24,28},{1,5},{5,9},{9,... | collective-permute-start | bytes 101384 | tf_op jit(solution)/shard_map/ppermute | solution.py:14
  17.9 4.7 %collective-permute-start.1 = (f32[33,1,256]{2,0,1:T(8,128)S(1)}, f32[33,1,256]{2,0,1:T(8,128)S(1)}, u32[]{:S(2)}, u32[]{:S(2)}) collective-permute-start(f32[33,1,256]{2,0,1:T(8,128)S(1)} %get-tuple-element.13), channel_id=1, source_target_pairs={{4,0},{8,4},{12,8},{16,12},{20,16},{24,20},{28,24},{5,1},{9,5},{13... | collective-permute-start | bytes 101384 | tf_op jit(solution)/shard_map/ppermute | solution.py:15
  26.6 8.9 %collective-permute-start.3 = (f32[33,66,1]{1,2,0:T(1,128)S(1)}, f32[33,66,1]{1,2,0:T(1,128)S(1)}, u32[]{:S(2)}, u32[]{:S(2)}) collective-permute-start(f32[33,66,1]{1,2,0:T(1,128)S(1)} %copy.32), channel_id=1, source_target_pairs={{1,0},{2,1},{3,2},{5,4},{6,5},{7,6},{9,8},{10,9},{11,10},{13,12},{... | collective-permute-start | bytes 26144 | tf_op jit(solution)/shard_map/ppermute | solution.py:15
  32.4 4.7 %collective-permute-start.2 = (f32[33,66,1]{1,2,0:T(1,128)S(1)}, f32[33,66,1]{1,2,0:T(1,128)S(1)}, u32[]{:S(2)}, u32[]{:S(2)}) collective-permute-start(f32[33,66,1]{1,2,0:T(1,128)S(1)} %copy.31), channel_id=1, source_target_pairs={{0,1},{1,2},{2,3},{4,5},{5,6},{6,7},{8,9},{9,10},{10,11},{12,13},{... | collective-permute-start | bytes 26144 | tf_op jit(solution)/shard_map/ppermute | solution.py:14
  38.8 1.7 copy-start
  38.8 1.9 copy-start.1
  38.8 2.6 %copy-start.2 = (f32[32,64,256]{2,1,0:T(8,128)S(1)}, f32[32,64,256]{2,1,0:T(8,128)}, u32[]{:S(2)}) copy-start(f32[32,64,256]{2,1,0:T(8,128)} %param.3) | copy-start | bytes 6291460
  41.3 7.0 %copy-start.3 = (f32[32,64,256]{2,0,1:T(8,128)S(1)}, f32[32,64,256]{2,0,1:T(8,128)}, u32[]{:S(2)}) copy-start(f32[32,64,256]{2,0,1:T(8,128)} %get-tuple-element.14) | copy-start | bytes 6291460
  48.3 10.7 %copy-start.4 = (f32[32,64,256]{2,0,1:T(8,128)S(1)}, f32[32,64,256]{2,0,1:T(8,128)}, u32[]{:S(2)}) copy-start(f32[32,64,256]{2,0,1:T(8,128)} %get-tuple-element.14) | copy-start | bytes 6291460
Sparse Core Ops, SparseCore 0:
  59.2 122.1 all-reduce.1
where the time goes:
time: 233 us
  waiting for transfers between devices  111 us (48%)
  other arithmetic  43.2 us (19%)
  local copies, waits for them, and re-layouts  30.4 us (13%)
  matrix products  21.4 us (9%)
  between operations  14.2 us (6%)
  starting transfers between devices  12.3 us (5%)
    psum x1, waiting for transfers between devices, on_device(): gram_total = lax.psum(inner_products(matrix, cell_count), ('gx', 'gy'))  108 us
    another operation x3, other arithmetic, on_device(): lower_tri = jnp.linalg.cholesky(gram_total)  12.4 us
    another operation x1, matrix products, on_device(): jax.scipy.linalg.solve_triangular(lower_tri, matrix, lower=True)  10.7 us
    dot_general x1, matrix products, inner_products(): jnp.dot(matrix, matrix.T, precision=lax.Precision.HIGHEST) / cell_count  10.7 us
    unnamed x13, local copies, waits for them, and re-layouts  9.88 us
    another operation x1, other arithmetic, on_device(): jax.scipy.linalg.solve_triangular(lower_tri, matrix, lower=True)  9.81 us
    concatenate x1, local copies, waits for them, and re-layouts, build_columns(): stacked = jnp.concatenate([center, along_x, along_y, react], 0)  9.01 us
    ppermute x2, starting transfers between devices, padded_2(): before = lax.ppermute(last, axis, up)  6.99 us
  transfers between devices with their start and end apart: 5, of which 2 were waited for; matrix products, arithmetic and copies ran while one was open for 8% of the time, Pallas kernels for 0%

commit v1 on v0

--- a/solution.py
+++ b/solution.py
@@ -43,7 +43,7 @@
     padded = padded_2(stacked, (("gx", 1), ("gy", 2)), 1)
     matrix = build_columns(padded[:modes_count], padded[modes_count], potential)
     cell_count = float(rows_here * cols_here * lax.axis_size("gx") * lax.axis_size("gy"))
-    gram_total = lax.psum(inner_products(matrix, cell_count), ("gx", "gy"))
+    gram_total = lax.psum(lax.psum(inner_products(matrix, cell_count), "gx"), "gy")
     lower_tri = jnp.linalg.cholesky(gram_total)
     basis_flat = jax.scipy.linalg.solve_triangular(lower_tri, matrix, lower=True)
     basis_field = basis_flat.reshape(basis_flat.shape[0], rows_here, cols_here)

time: 233 us -> 216 us (0.927); the launches traced: 233 us -> 213 us
  waiting for transfers between devices: 111 us -> 91.1 us
    psum x1 -> x2, waiting for transfers between devices: 108 us -> 87.6 us  [the longest x1 68.2 us: on_device(): lax.psum(inner_products(matrix, cell_count), 'gx')]
  transfers between devices with their start and end apart: 5 -> 6, of which waited for: 2 -> 3; matrix products, arithmetic and copies ran while one was open for 8% -> 9% of each run, Pallas kernels for 0% -> 0%
where the time goes in v1:
time: 216 us; the launch traced here: 213 us
  waiting for transfers between devices  91.1 us (42%)
  other arithmetic  43.2 us (20%)
  local copies, waits for them, and re-layouts  30.4 us (14%)
  matrix products  21.4 us (10%)
  between operations  14.2 us (7%)
  starting transfers between devices  12.6 us (6%)
    psum x1, waiting for transfers between devices, on_device(): lax.psum(inner_products(matrix, cell_count), 'gx')  68.2 us
    psum x1, waiting for transfers between devices, on_device(): lax.psum(lax.psum(inner_products(matrix, cell_count), 'gx'), 'gy')  19.5 us
    another operation x3, other arithmetic, on_device(): lower_tri = jnp.linalg.cholesky(gram_total)  12.4 us
    another operation x1, matrix products, on_device(): jax.scipy.linalg.solve_triangular(lower_tri, matrix, lower=True)  10.7 us
    dot_general x1, matrix products, inner_products(): jnp.dot(matrix, matrix.T, precision=lax.Precision.HIGHEST) / cell_count  10.7 us
    unnamed x13, local copies, waits for them, and re-layouts  9.88 us
    another operation x1, other arithmetic, on_device(): jax.scipy.linalg.solve_triangular(lower_tri, matrix, lower=True)  9.81 us
    concatenate x1, local copies, waits for them, and re-layouts, build_columns(): stacked = jnp.concatenate([center, along_x, along_y, react], 0)  9.01 us
  transfers between devices with their start and end apart: 6, of which 3 were waited for; matrix products, arithmetic and copies ran while one was open for 9% of the time, Pallas kernels for 0%

profile of v1, /device:TPU:1, one launch (start us, length us, event | category | flops | bytes accessed | tf_op | source)
XLA Modules:
  0.0 212.9 jit_solution(1584138746007479680)
XLA Ops:
  7.2 0.9 broadcast_in_dim.3
  8.1 5.0 %fusion.22 = (f32[32,64,256]{2,0,1:T(8,128)}, f32[33,64,256]{2,0,1:T(8,128)S(1)}, f32[32,64,256]{2,0,1:T(8,128)}) fusion(f32[32,64,256]{2,1,0:T(8,128)} %param.3, f32[64,256]{1,0:T(8,128)} %param.5), kind=kLoop, calls=%fused_computation.51 | loop fusion | flops 524287 | bytes 8454144 | tf_op args[0]
  13.1 0.9 dynamic-update-slice.4
  14.0 3.9 %collective-permute-start = (f32[33,1,256]{2,0,1:T(8,128)S(1)}, f32[33,1,256]{2,0,1:T(8,128)S(1)}, u32[]{:S(2)}, u32[]{:S(2)}) collective-permute-start(f32[33,1,256]{2,0,1:T(8,128)S(1)} %get-tuple-element.12), channel_id=1, source_target_pairs={{0,4},{4,8},{8,12},{12,16},{16,20},{20,24},{24,28},{1,5},{5,9},{9,... | collective-permute-start | bytes 101384 | tf_op jit(solution)/shard_map/ppermute | solution.py:14
  17.9 1.3 collective-permute-start.1
  19.2 3.4 %collective-permute-done.1 = f32[33,1,256]{2,0,1:T(8,128)S(1)} collective-permute-done((f32[33,1,256]{2,0,1:T(8,128)S(1)}, f32[33,1,256]{2,0,1:T(8,128)S(1)}, u32[]{:S(2)}, u32[]{:S(2)}) %collective-permute-start.1) | collective-permute-done | bytes 33824 | tf_op jit(solution)/shard_map/ppermute | solution.py:15
  22.8 1.9 fusion.20
  24.8 1.8 copy.32
  26.6 4.0 %collective-permute-start.3 = (f32[33,66,1]{1,2,0:T(1,128)S(1)}, f32[33,66,1]{1,2,0:T(1,128)S(1)}, u32[]{:S(2)}, u32[]{:S(2)}) collective-permute-start(f32[33,66,1]{1,2,0:T(1,128)S(1)} %copy.32), channel_id=1, source_target_pairs={{1,0},{2,1},{3,2},{5,4},{6,5},{7,6},{9,8},{10,9},{11,10},{13,12},{... | collective-permute-start | bytes 26144 | tf_op jit(solution)/shard_map/ppermute | solution.py:15
  30.6 1.8 copy.31
  32.4 3.1 %collective-permute-start.2 = (f32[33,66,1]{1,2,0:T(1,128)S(1)}, f32[33,66,1]{1,2,0:T(1,128)S(1)}, u32[]{:S(2)}, u32[]{:S(2)}) collective-permute-start(f32[33,66,1]{1,2,0:T(1,128)S(1)} %copy.31), channel_id=1, source_target_pairs={{0,1},{1,2},{2,3},{4,5},{5,6},{6,7},{8,9},{9,10},{10,11},{12,13},{... | collective-permute-start | bytes 26144 | tf_op jit(solution)/shard_map/ppermute | solution.py:14
  35.4 1.7 copy.34
  37.1 1.7 copy.33
  38.8 1.5 pad_maximum_fusion.10
  40.5 0.2 copy-done.1
  40.7 0.7 copy-done.2
  41.3 7.0 %fusion.9 = (f32[32,64,256]{2,0,1:T(8,128)}, f32[32,64,256]{2,0,1:T(8,128)}) fusion(f32[33,64,256]{2,0,1:T(8,128)S(1)} %dynamic-update-slice.4, f32[33,1,256]{2,0,1:T(8,128)S(1)} %collective-permute-done, f32[33,1,256]{2,0,1:T(8,128)S(1)} %collective-permute-done.1, f32[64,256]{1,0:T(8,128)S(1)} %get-tuple-element.19, f32[64,256]{1,0:T(8,128)S(1)} %get-tuple-element.17, ...), kind=kLoop, calls=%fused_computation.18 | loop fusion | flops 9437184 | bytes 8801296 | tf_op jit(solution)/shard_map/add | solution.py:27
  48.3 10.7 %fusion.12 = f32[128,128]{0,1:T(8,128)} fusion(f32[32,64,256]{2,0,1:T(8,128)} %get-tuple-element.16, f32[32,64,256]{2,0,1:T(8,128)} %get-tuple-element.9, f32[32,64,256]{2,0,1:T(8,128)} %get-tuple-element.8, f32[32,64,256]{2,0,1:T(8,128)S(1)} %copy-done.3), kind=kOutput, calls=%fused_computation.23 | convolution fusion | flops 3227533312 | bytes 8454144 | tf_op jit(solution)/shard_map/dot_general | solution.py:35
  59.0 0.2 all-reduce.5.cloned.1.call-start
  59.3 68.2 %all-reduce.3.cloned.1.call-done = f32[128,128]{0,1:T(8,128)} async-done(((f32[128,128]{0,1:T(8,128)}), f32[128,128]{0,1:T(8,128)}) %all-reduce.3.cloned.1.call-update) | async-done | bytes 65552 | tf_op jit(solution)/shard_map/psum | solution.py:46
  127.5 5.7 %pad_maximum_fusion = f32[128,64,256]{2,0,1:T(8,128)} fusion(f32[32,64,256]{2,0,1:T(8,128)} %get-tuple-element.16, f32[32,64,256]{2,0,1:T(8,128)} %get-tuple-element.9, f32[32,64,256]{2,0,1:T(8,128)} %get-tuple-element.8, f32[32,64,256]{2,0,1:T(8,128)S(1)} %copy-done.4), kind=kLoop, calls=%fused_computation | loop fusion | flops 6291456 | bytes 16777216 | tf_op jit(solution)/shard_map/concatenate | solution.py:30
  133.2 9.0 %copy.45 = f32[128,64,256]{0,2,1:T(8,128)} copy(f32[128,64,256]{2,0,1:T(8,128)} %pad_maximum_fusion) | data formatting | bytes 16777216 | tf_op jit(solution)/shard_map/concatenate | solution.py:30
  142.2 19.5 %all-reduce.5.cloned.1.call-done = f32[128,128]{0,1:T(8,128)} async-done(((f32[128,128]{0,1:T(8,128)}), f32[128,128]{0,1:T(8,128)}) %all-reduce.5.cloned.1.call-update) | async-done | bytes 65552 | tf_op jit(solution)/shard_map/psum | solution.py:46
  161.7 0.9 copy.44
  162.6 0.9 fusion.18
  163.4 11.7 %cholesky.16 = f32[128,128]{1,0:T(8,128)S(1)} custom-call(f32[128,128]{1,0:T(8,128)S(1)} %fusion.18), custom_call_target="Cholesky" | custom-call | tf_op jit(solution)/shard_map/jit(cholesky)/cholesky | solution.py:47
  175.2 0.6 compare_reduce_fusion
  175.8 0.7 fusion.19
  176.5 0.7 copy.48
  177.2 9.8 %custom-call.7 = f32[1,128,128]{1,2,0:T(8,128)S(1)} custom-call(f32[1,128,128]{2,1,0:T(8,128)S(1)} %get-tuple-element.22), custom_call_target="InvertDiagBlocksLowerTriangular" | custom-call | tf_op jit(solution)/shard_map/jit(_solve_triangular)/triangular_solve | solution.py:48
  187.0 10.7 %fusion = f32[128,64,256]{2,0,1:T(8,128)S(1)} fusion(f32[128,64,256]{0,2,1:T(8,128)} %copy.45, f32[1,128,128]{1,2,0:T(8,128)S(1)} %custom-call.7), kind=kOutput, calls=%fused_computation.1 | convolution fusion | flops 3221225472 | bytes 16842752 | tf_op jit(solution)/shard_map/jit(_solve_triangular)/triangular_solve | solution.py:48
  197.8 8.3 %copy.47 = f32[128,64,256]{2,1,0:T(8,128)} copy(f32[128,64,256]{2,0,1:T(8,128)S(1)} %fusion) | data formatting | bytes 16777216
  (19 shorter events, 0.5 us)
Async XLA Ops:
  7.2 120.3 %all-reduce.3.cloned.1.call-start = ((), (), s32[]{:S(2)}) async-start(), calls=%async_computation | async-start | bytes 131072 | tf_op jit(solution)/shard_map/psum | solution.py:46
  14.0 5.2 %collective-permute-start = (f32[33,1,256]{2,0,1:T(8,128)S(1)}, f32[33,1,256]{2,0,1:T(8,128)S(1)}, u32[]{:S(2)}, u32[]{:S(2)}) collective-permute-start(f32[33,1,256]{2,0,1:T(8,128)S(1)} %get-tuple-element.12), channel_id=1, source_target_pairs={{0,4},{4,8},{8,12},{12,16},{16,20},{20,24},{24,28},{1,5},{5,9},{9,... | collective-permute-start | bytes 101384 | tf_op jit(solution)/shard_map/ppermute | solution.py:14
  17.9 4.7 %collective-permute-start.1 = (f32[33,1,256]{2,0,1:T(8,128)S(1)}, f32[33,1,256]{2,0,1:T(8,128)S(1)}, u32[]{:S(2)}, u32[]{:S(2)}) collective-permute-start(f32[33,1,256]{2,0,1:T(8,128)S(1)} %get-tuple-element.13), channel_id=1, source_target_pairs={{4,0},{8,4},{12,8},{16,12},{20,16},{24,20},{28,24},{5,1},{9,5},{13... | collective-permute-start | bytes 101384 | tf_op jit(solution)/shard_map/ppermute | solution.py:15
  26.6 8.9 %collective-permute-start.3 = (f32[33,66,1]{1,2,0:T(1,128)S(1)}, f32[33,66,1]{1,2,0:T(1,128)S(1)}, u32[]{:S(2)}, u32[]{:S(2)}) collective-permute-start(f32[33,66,1]{1,2,0:T(1,128)S(1)} %copy.32), channel_id=1, source_target_pairs={{1,0},{2,1},{3,2},{5,4},{6,5},{7,6},{9,8},{10,9},{11,10},{13,12},{... | collective-permute-start | bytes 26144 | tf_op jit(solution)/shard_map/ppermute | solution.py:15
  32.4 4.7 %collective-permute-start.2 = (f32[33,66,1]{1,2,0:T(1,128)S(1)}, f32[33,66,1]{1,2,0:T(1,128)S(1)}, u32[]{:S(2)}, u32[]{:S(2)}) collective-permute-start(f32[33,66,1]{1,2,0:T(1,128)S(1)} %copy.31), channel_id=1, source_target_pairs={{0,1},{1,2},{2,3},{4,5},{5,6},{6,7},{8,9},{9,10},{10,11},{12,13},{... | collective-permute-start | bytes 26144 | tf_op jit(solution)/shard_map/ppermute | solution.py:14
  38.8 1.7 copy-start
  38.8 1.9 copy-start.1
  38.8 2.6 %copy-start.2 = (f32[32,64,256]{2,1,0:T(8,128)S(1)}, f32[32,64,256]{2,1,0:T(8,128)}, u32[]{:S(2)}) copy-start(f32[32,64,256]{2,1,0:T(8,128)} %param.3) | copy-start | bytes 6291460
  41.3 7.0 %copy-start.3 = (f32[32,64,256]{2,0,1:T(8,128)S(1)}, f32[32,64,256]{2,0,1:T(8,128)}, u32[]{:S(2)}) copy-start(f32[32,64,256]{2,0,1:T(8,128)} %get-tuple-element.14) | copy-start | bytes 6291460
  48.3 79.1 %copy-start.4 = (f32[32,64,256]{2,0,1:T(8,128)S(1)}, f32[32,64,256]{2,0,1:T(8,128)}, u32[]{:S(2)}) copy-start(f32[32,64,256]{2,0,1:T(8,128)} %get-tuple-element.14) | copy-start | bytes 6291460
  59.0 102.6 %all-reduce.5.cloned.1.call-start = ((), (), s32[]{:S(2)}) async-start(), calls=%async_computation.1 | async-start | bytes 131072 | tf_op jit(solution)/shard_map/psum | solution.py:46
Sparse Core Ops, SparseCore 0:
  59.2 68.2 all-reduce.2
  129.7 31.8 all-reduce.4
